TPU v7x, 32 devices: a whole 2x2x4 slice. The times are simulated.
32 devices in a mesh: cells: 8 (over y, x, core), genes: 4 (over z).
Axes of the slice: x: 2, y: 2, z: 4, core: 2. Of those that a mesh axis runs over, the one named last changes fastest.
Arguments:
- counts: int32 [8192, 4096], P('cells', 'genes'), may hold values from 0 to 26, as said below
- library: int32 [8192], P('cells'), may hold values from 2000 to 19999
Outputs:
- adjacency: float32 [4096, 4096], P('cells', 'genes')
- connectivity: float32 [4096], P('cells')
Inputs may be any that keep to these rules, and one draw needn't show every extreme that they name: Non-negative integer counts.
All inputs are finite; a program needn't handle non-finite values.
Results may differ from a plain program's by a relative error of at most 0.006.
Values may be sent and summed in bfloat16 or wider, within the bound.
A program may use at most 128 MiB of HBM per device.

v0:
```python
import jax
import jax.numpy as jnp
from jax import lax
from jax.sharding import PartitionSpec as P


def normalize(counts, library):
    factor = 10000.0 / library.astype(jnp.float32)
    return jnp.log1p(counts.astype(jnp.float32) * factor[:, None]).astype(jnp.bfloat16)


def cross_product(left, right):
    return lax.dot_general(
        left, right, (((0,), (0,)), ((), ())), preferred_element_type=jnp.float32
    )


def shards(counts, library):
    own_block = normalize(counts, library)
    col_width = own_block.shape[1]
    cell_groups = lax.axis_size("cells")
    gene_total = col_width * lax.axis_size("genes")
    row_width = gene_total // cell_groups
    total_cells = float(counts.shape[0] * cell_groups)
    widened = own_block.astype(jnp.float32)
    local_sums = jnp.sum(widened, axis=0)
    local_squares = jnp.sum(widened * widened, axis=0)
    block_sums, block_squares = lax.psum((local_sums, local_squares), "cells")
    gene_sums, gene_squares = (
        lax.all_gather(block_sums, "genes", axis=0, tiled=True),
        lax.all_gather(block_squares, "genes", axis=0, tiled=True),
    )
    full_block = lax.all_gather(own_block, "genes", axis=1, tiled=True)
    gram_tile = lax.psum_scatter(
        cross_product(full_block, own_block), "cells", scatter_dimension=0, tiled=True
    )
    means = gene_sums / total_cells
    variances = gene_squares / total_cells - means * means
    scales = lax.rsqrt(variances + 1e-05)
    row_first = lax.axis_index("cells") * row_width
    col_first = lax.axis_index("genes") * col_width
    row_means = lax.dynamic_slice_in_dim(means, row_first, row_width, 0)
    col_means = lax.dynamic_slice_in_dim(means, col_first, col_width, 0)
    row_scales = lax.dynamic_slice_in_dim(scales, row_first, row_width, 0)
    col_scales = lax.dynamic_slice_in_dim(scales, col_first, col_width, 0)
    correlation = (
        (gram_tile / total_cells - row_means[:, None] * col_means[None, :])
        * row_scales[:, None]
        * col_scales[None, :]
    )
    powered = correlation**6
    row_index = row_first + jnp.arange(row_width, dtype=jnp.int32)[:, None]
    col_index = col_first + jnp.arange(col_width, dtype=jnp.int32)[None, :]
    adjacency = jnp.where(row_index == col_index, jnp.float32(0.0), powered)
    connectivity = lax.psum(jnp.sum(adjacency, axis=1), "genes")
    return (adjacency, connectivity)


def solution(mesh):
    return jax.shard_map(
        shards,
        mesh=mesh,
        in_specs=(P("cells", "genes"), P("cells")),
        out_specs=(P("cells", "genes"), P("cells")),
        check_vma=False,
    )
```

profile of v0, /device:TPU:0, one launch (start us, length us, event | category | flops | bytes accessed | tf_op | source)
XLA Modules:
  0.0 318.0 jit_solution(6613592547870994486)
XLA Ops:
  7.2 0.0 all-gather.2.cloned.1.call-start
  7.2 0.7 convert_divide_fusion
  7.9 5.6 %convert_reduce_fusion = (f32[1024]{0:T(1024)S(1)}, f32[1024]{0:T(1024)S(1)}, bf16[1024,1024]{1,0:T(8,128)(2,1)}) fusion(f32[1024]{0:T(1024)S(1)} %convert_divide_fusion, s32[1024,1024]{1,0:T(8,128)} %param.2), kind=kLoop, calls=%fused_computation.1 | loop fusion | flops 7337984 | bytes 6303744 | tf_op jit(solution)/shard_map/reduce_sum | solution.py:26
  13.5 0.0 copy-start
  13.5 0.0 all-gather.2.cloned.1.call-update
  13.5 0.0 reduce-scatter.2.cloned.1.call-start
  13.5 152.4 %all-gather.2.cloned.1.call-done = bf16[1024,4096]{1,0:T(8,128)(2,1)} async-done(((bf16[1024,1024]{1,0:T(8,128)(2,1)}), bf16[1024,4096]{1,0:T(8,128)(2,1)}) %all-gather.2.cloned.1.call-update) | async-done | bytes 8388624 | tf_op jit(solution)/shard_map/all_gather | solution.py:33
  166.0 0.0 copy-done
  166.0 14.6 %fusion.4 = f32[4096,1024]{1,0:T(8,128)} fusion(bf16[1024,4096]{1,0:T(8,128)(2,1)} %all-gather.2.cloned.1.call-done, bf16[1024,1024]{1,0:T(8,128)(2,1)S(1)} %copy-done), kind=kOutput, calls=%fused_computation.12 | convolution fusion | flops 8589934592 | bytes 27262976 | tf_op jit(solution)/shard_map/dot_general | solution.py:13
  180.6 0.0 reduce-scatter.2.cloned.1.call-update
  180.7 14.0 %all-reduce = (f32[1024]{0:T(1024)S(1)}, f32[1024]{0:T(1024)S(1)}) all-reduce(f32[1024]{0:T(1024)S(1)} %get-tuple-element.3, f32[1024]{0:T(1024)S(1)} %get-tuple-element.2), channel_id=1, replica_groups=mesh['cells'=8,'genes'=4] {'cells'}, use_global_device_ids=true, to_apply=%region_4.0 | all-reduce | flops 2048 | bytes 16384 | tf_op jit(solution)/shard_map/psum | solution.py:28
  194.7 13.2 %all_gather.10 = f32[4096]{0:T(1024)S(1)} all-gather(f32[1024]{0:T(1024)S(1)} %get-tuple-element.5), channel_id=1, replica_groups=mesh['cells'=8,'genes'=4] {'genes'}, dimensions={0}, use_global_device_ids=true | all-gather | bytes 20480 | tf_op jit(solution)/shard_map/all_gather | solution.py:30
  207.9 13.2 %all_gather.11 = f32[4096]{0:T(1024)S(1)} all-gather(f32[1024]{0:T(1024)S(1)} %get-tuple-element.4), channel_id=1, replica_groups=mesh['cells'=8,'genes'=4] {'genes'}, dimensions={0}, use_global_device_ids=true | all-gather | bytes 20480 | tf_op jit(solution)/shard_map/all_gather | solution.py:31
  221.1 0.1 dynamic_slice.12
  221.2 0.1 dynamic_slice.14
  221.3 73.9 %reduce-scatter.2.cloned.1.call-done = f32[512,1024]{1,0:T(8,128)} async-done(((f32[4096,1024]{1,0:T(8,128)}), f32[512,1024]{1,0:T(8,128)}) %reduce-scatter.2.cloned.1.call-update) | async-done | bytes 2097168 | tf_op jit(solution)/shard_map/reduce_scatter | solution.py:34
  295.2 3.8 %fusion.2 = (f32[512]{0:T(512)S(1)}, f32[512,1024]{1,0:T(8,128)}) fusion(f32[1024]{0:T(1024)S(1)} %dynamic_slice.15, f32[512]{0:T(512)S(1)} %dynamic_slice.14, f32[1024]{0:T(1024)S(1)} %dynamic_slice.13, f32[512]{0:T(512)S(1)} %dynamic_slice.12, f32[512,1024]{1,0:T(8,128)} %reduce-scatter.2.cloned.1.call-done, s32[1024]{0:T(1024)S(1)} %iota_add_fusion, ...), kind=kLoop, calls=%fused_computation.11 | loop fusion | flops 5766656 | bytes 4214784 | tf_op jit(solution)/shard_map/reduce_sum | solution.py:55
  299.0 12.2 %psum.23 = f32[512]{0:T(512)} all-reduce(f32[512]{0:T(512)S(1)} %get-tuple-element.6), channel_id=1, replica_groups=mesh['cells'=8,'genes'=4] {'genes'}, use_global_device_ids=true, to_apply=%region_6.7 | all-reduce | flops 512 | bytes 4096 | tf_op jit(solution)/shard_map/psum | solution.py:55
  (5 shorter events, 0.0 us)
Async XLA Ops:
  7.2 158.8 %all-gather.2.cloned.1.call-start = ((), (), s32[]{:S(2)}) async-start(), calls=%async_computation.1 | async-start | bytes 10485760 | tf_op jit(solution)/shard_map/all_gather | solution.py:33
  13.5 152.5 %copy-start = (bf16[1024,1024]{1,0:T(8,128)(2,1)S(1)}, bf16[1024,1024]{1,0:T(8,128)(2,1)}, u32[]{:S(2)}) copy-start(bf16[1024,1024]{1,0:T(8,128)(2,1)} %get-tuple-element.8) | copy-start | bytes 6291460
  13.5 281.7 %reduce-scatter.2.cloned.1.call-start = ((), (), s32[]{:S(2)}) async-start(), calls=%async_computation.2 | async-start | bytes 18874368 | tf_op jit(solution)/shard_map/reduce_scatter | solution.py:34
Sparse Core Ops, SparseCore 0:
  13.6 152.3 all-gather.1
  180.8 114.3 reduce-scatter.1
where the time goes:
time: 318 us
  waiting for transfers between devices  226 us (71%)
  blocking collectives  52.7 us (17%)
  matrix products  14.6 us (5%)
  between operations  14.1 us (4%)
  other arithmetic  10 us (3%)
    all_gather x1, waiting for transfers between devices, shards(): full_block = lax.all_gather(own_block, 'genes', axis=1, tiled=True)  152 us
    reduce_scatter x1, waiting for transfers between devices, shards(): lax.psum_scatter(cross_product(full_block, own_block), 'cells', scatter_d...  73.9 us
    dot_general x1, matrix products, cross_product(): lax.dot_general(left, right, (((0,), (0,)), ((), ())), preferred_element_...  14.6 us
    psum x1, blocking collectives, shards(): block_sums, block_squares = lax.psum((local_sums, local_squares), 'cells')  14 us
    all_gather x1, blocking collectives, shards(): lax.all_gather(block_sums, 'genes', axis=0, tiled=True)  13.2 us
    all_gather x1, blocking collectives, shards(): lax.all_gather(block_squares, 'genes', axis=0, tiled=True)  13.2 us
    psum x1, blocking collectives, shards(): connectivity = lax.psum(jnp.sum(adjacency, axis=1), 'genes')  12.2 us
  transfers between devices with their start and end apart: 2, of which 2 were waited for; matrix products, arithmetic and copies ran while one was open for 0% of the time, Pallas kernels for 0%

commit v1 on v0

v1 whole, which is shorter than its diff:
```python
import jax
import jax.numpy as jnp
from jax import lax
from jax.sharding import PartitionSpec as P

CHUNKS = 4
DEPTH = 3


def normalize(counts, library):
    factor = 10000.0 / library.astype(jnp.float32)
    return jnp.log1p(counts.astype(jnp.float32) * factor[:, None]).astype(jnp.bfloat16)


def shards(counts, library):
    own_block = normalize(counts, library)
    cells, col_width = own_block.shape
    cell_groups = lax.axis_size("cells")
    gene_groups = lax.axis_size("genes")
    row_width = col_width * gene_groups // cell_groups
    owners = col_width // row_width
    part = row_width // CHUNKS
    total_cells = float(cells * cell_groups)
    me = lax.axis_index("genes")
    ring = [(i, (i + 1) % gene_groups) for i in range(gene_groups)]

    split = own_block.reshape(cells, owners, CHUNKS, part)
    flights = []
    blocks = []
    for q in range(CHUNKS):
        held = split[:, :, q, :].reshape(cells, owners * part)
        mine = [held]
        for step in range(gene_groups - 1):
            if len(flights) >= DEPTH:
                held, flights[-DEPTH] = lax.optimization_barrier((held, flights[-DEPTH]))
            held = lax.ppermute(held, "genes", ring)
            flights.append(held)
            mine.append(held)
        blocks.append(mine)

    widened = own_block.astype(jnp.float32)
    sums = jnp.stack([jnp.sum(widened, axis=0), jnp.sum(widened * widened, axis=0)])
    sums = lax.psum(sums, "cells")
    all_sums = lax.all_gather(sums, "genes", axis=1, tiled=True)

    pieces = []
    for q in range(CHUNKS):
        tiles = jnp.zeros((gene_groups, owners * part, col_width), jnp.float32)
        for step in range(gene_groups):
            source = lax.rem(me - step + gene_groups, gene_groups)
            tile = lax.dot_general(
                blocks[q][step], own_block, (((0,), (0,)), ((), ())), preferred_element_type=jnp.float32
            )
            tiles = lax.dynamic_update_slice(tiles, tile[None], (source, 0, 0))
        tiles = tiles.reshape(cell_groups * part, col_width)
        pieces.append(lax.psum_scatter(tiles, "cells", scatter_dimension=0, tiled=True))
    gram_tile = jnp.concatenate(pieces, axis=0)

    means = all_sums[0] / total_cells
    variances = all_sums[1] / total_cells - means * means
    scales = lax.rsqrt(variances + 1e-05)
    row_first = lax.axis_index("cells") * row_width
    col_first = me * col_width
    row_means = lax.dynamic_slice_in_dim(means, row_first, row_width, 0)
    col_means = lax.dynamic_slice_in_dim(means, col_first, col_width, 0)
    row_scales = lax.dynamic_slice_in_dim(scales, row_first, row_width, 0)
    col_scales = lax.dynamic_slice_in_dim(scales, col_first, col_width, 0)
    correlation = (
        (gram_tile / total_cells - row_means[:, None] * col_means[None, :])
        * row_scales[:, None]
        * col_scales[None, :]
    )
    powered = correlation**6
    row_index = row_first + jnp.arange(row_width, dtype=jnp.int32)[:, None]
    col_index = col_first + jnp.arange(col_width, dtype=jnp.int32)[None, :]
    adjacency = jnp.where(row_index == col_index, jnp.float32(0.0), powered)
    connectivity = lax.psum(jnp.sum(adjacency, axis=1), "genes")
    return (adjacency, connectivity)


def solution(mesh):
    return jax.shard_map(
        shards,
        mesh=mesh,
        in_specs=(P("cells", "genes"), P("cells")),
        out_specs=(P("cells", "genes"), P("cells")),
        check_vma=False,
    )
```

time: 318 us -> 303 us (0.953)
  waiting for transfers between devices: 226 us -> 196 us
  local copies, waits for them, and re-layouts: 0.17 us -> 17.1 us
  blocking collectives: 52.7 us -> 38.3 us
  matrix products: 14.6 us -> 25.9 us
  starting transfers between devices: 0.08 us -> 3.41 us
    all_gather x1 -> x0, waiting for transfers between devices: 152 us -> none  [shards(): full_block = lax.all_gather(own_block, 'genes', axis=1, tiled=True)]
    ppermute x0 -> x12, waiting for transfers between devices: none -> 135 us  [shards(): held = lax.ppermute(held, 'genes', ring)]
    reduce_scatter x1 -> x4, waiting for transfers between devices: 73.9 us -> 60 us  [shards(): lax.psum_scatter(tiles, 'cells', scatter_dimension=0, tiled=True)]
    all_gather x2 -> x1, blocking collectives: 26.4 us -> 13.1 us  [shards(): all_sums = lax.all_gather(sums, 'genes', axis=1, tiled=True)]
    dot_general x1 -> x16, matrix products: 14.6 us -> 25.9 us  [shards(): lax.dot_general(blocks[q][step], own_block, (((0,), (0,)), ((), ())), pre...]
    unnamed x2 -> x11, local copies, waits for them, and re-layouts: 0.01 us -> 8.11 us
    another operation x0 -> x4, local copies, waits for them, and re-layouts: none -> 7.97 us
    ppermute x0 -> x12, starting transfers between devices: none -> 3.25 us  [shards(): held = lax.ppermute(held, 'genes', ring)]
  transfers between devices with their start and end apart: 2 -> 16, of which waited for: 2 -> 14; matrix products, arithmetic and copies ran while one was open for 0% -> 11% of each run, Pallas kernels for 0% -> 0%
where the time goes in v1:
time: 303 us; the launch traced here: 302 us
  waiting for transfers between devices  196 us (65%)
  blocking collectives  38.3 us (13%)
  matrix products  25.9 us (9%)
  local copies, waits for them, and re-layouts  17.1 us (6%)
  between operations  13.9 us (5%)
  other arithmetic  8 us (3%)
  starting transfers between devices  3.41 us (1%)
    ppermute x12, waiting for transfers between devices, shards(): held = lax.ppermute(held, 'genes', ring)  135 us
    reduce_scatter x4, waiting for transfers between devices, shards(): lax.psum_scatter(tiles, 'cells', scatter_dimension=0, tiled=True)  60 us
    dot_general x16, matrix products, shards(): lax.dot_general(blocks[q][step], own_block, (((0,), (0,)), ((), ())), pre...  25.9 us
    all_gather x1, blocking collectives, shards(): all_sums = lax.all_gather(sums, 'genes', axis=1, tiled=True)  13.1 us
    psum x1, blocking collectives, shards(): sums = lax.psum(sums, 'cells')  12.9 us
    psum x1, blocking collectives, shards(): connectivity = lax.psum(jnp.sum(adjacency, axis=1), 'genes')  12.3 us
    unnamed x11, local copies, waits for them, and re-layouts  8.11 us
    another operation x4, local copies, waits for them, and re-layouts  7.97 us
  transfers between devices with their start and end apart: 16, of which 14 were waited for; matrix products, arithmetic and copies ran while one was open for 11% of the time, Pallas kernels for 0%

profile of v1, /device:TPU:0, one launch (start us, length us, event | category | flops | bytes accessed | tf_op | source)
XLA Modules:
  0.0 302.3 jit_solution(8457469932036976661)
XLA Ops:
  7.2 5.4 %copy.4 = s32[1024,1024]{0,1:T(8,128)} copy(s32[1024,1024]{1,0:T(8,128)} %param.2) | data formatting | bytes 8388608 | tf_op args[0]
  12.6 4.2 %convert_reduce_fusion = (f32[1024]{0:T(1024)S(1)}, f32[1024]{0:T(1024)S(1)}, bf16[1024,1024]{0,1:T(8,128)(2,1)S(1)}) fusion(f32[1024]{0:T(1024)S(1)} %convert_divide_fusion, s32[1024,1024]{0,1:T(8,128)} %copy.4), kind=kLoop, calls=%fused_computation.1 | loop fusion | flops 7337984 | bytes 6303744 | tf_op jit(solution)/shard_map/reduce_sum | solution.py:42
  18.7 3.1 %collective-permute-start = (bf16[1024,256]{0,1:T(8,128)(2,1)S(1)}, bf16[1024,256]{0,1:T(8,128)(2,1)}, u32[]{:S(2)}, u32[]{:S(2)}) collective-permute-start(bf16[1024,256]{0,1:T(8,128)(2,1)S(1)} %bitcast.119), channel_id=1, source_target_pairs={{0,1},{1,2},{2,3},{3,0},{4,5},{5,6},{6,7},{7,4},{8,9},{9,10},{10,1... | collective-permute-start | bytes 1572872 | tf_op jit(solution)/shard_map/ppermute | solution.py:36
  21.7 14.1 %collective-permute-done = bf16[1024,256]{0,1:T(8,128)(2,1)} collective-permute-done((bf16[1024,256]{0,1:T(8,128)(2,1)S(1)}, bf16[1024,256]{0,1:T(8,128)(2,1)}, u32[]{:S(2)}, u32[]{:S(2)}) %collective-permute-start) | collective-permute-done | bytes 524320 | tf_op jit(solution)/shard_map/ppermute | solution.py:36
  35.8 2.5 broadcast.33.clone.3
  40.0 11.0 %collective-permute-done.1 = bf16[1024,256]{0,1:T(8,128)(2,1)} collective-permute-done((bf16[1024,256]{0,1:T(8,128)(2,1)}, bf16[1024,256]{0,1:T(8,128)(2,1)}, u32[]{:S(2)}, u32[]{:S(2)}) %collective-permute-start.1) | collective-permute-done | bytes 524320 | tf_op jit(solution)/shard_map/ppermute | solution.py:36
  51.0 2.8 fusion.20
  53.8 2.8 fusion.19
  56.5 8.7 %collective-permute-done.2 = bf16[1024,256]{0,1:T(8,128)(2,1)S(1)} collective-permute-done((bf16[1024,256]{0,1:T(8,128)(2,1)}, bf16[1024,256]{0,1:T(8,128)(2,1)S(1)}, u32[]{:S(2)}, u32[]{:S(2)}) %collective-permute-start.2) | collective-permute-done | bytes 524320 | tf_op jit(solution)/shard_map/ppermute | solution.py:36
  67.1 13.4 %collective-permute-done.3 = bf16[1024,256]{0,1:T(8,128)(2,1)S(1)} collective-permute-done((bf16[1024,256]{0,1:T(8,128)(2,1)}, bf16[1024,256]{0,1:T(8,128)(2,1)S(1)}, u32[]{:S(2)}, u32[]{:S(2)}) %collective-permute-start.3) | collective-permute-done | bytes 524320 | tf_op jit(solution)/shard_map/ppermute | solution.py:36
  84.7 8.1 %collective-permute-done.4 = bf16[1024,256]{0,1:T(8,128)(2,1)S(1)} collective-permute-done((bf16[1024,256]{0,1:T(8,128)(2,1)S(1)}, bf16[1024,256]{0,1:T(8,128)(2,1)S(1)}, u32[]{:S(2)}, u32[]{:S(2)}) %collective-permute-start.4) | collective-permute-done | bytes 524320 | tf_op jit(solution)/shard_map/ppermute | solution.py:36
  96.3 8.0 %collective-permute-done.5 = bf16[1024,256]{0,1:T(8,128)(2,1)S(1)} collective-permute-done((bf16[1024,256]{0,1:T(8,128)(2,1)S(1)}, bf16[1024,256]{0,1:T(8,128)(2,1)S(1)}, u32[]{:S(2)}, u32[]{:S(2)}) %collective-permute-start.5) | collective-permute-done | bytes 524320 | tf_op jit(solution)/shard_map/ppermute | solution.py:36
  106.1 12.7 %collective-permute-done.6 = bf16[1024,256]{0,1:T(8,128)(2,1)S(1)} collective-permute-done((bf16[1024,256]{0,1:T(8,128)(2,1)S(1)}, bf16[1024,256]{0,1:T(8,128)(2,1)S(1)}, u32[]{:S(2)}, u32[]{:S(2)}) %collective-permute-start.6) | collective-permute-done | bytes 524320 | tf_op jit(solution)/shard_map/ppermute | solution.py:36
  123.2 9.6 %collective-permute-done.7 = bf16[1024,256]{0,1:T(8,128)(2,1)S(1)} collective-permute-done((bf16[1024,256]{0,1:T(8,128)(2,1)S(1)}, bf16[1024,256]{0,1:T(8,128)(2,1)S(1)}, u32[]{:S(2)}, u32[]{:S(2)}) %collective-permute-start.7) | collective-permute-done | bytes 524320 | tf_op jit(solution)/shard_map/ppermute | solution.py:36
  136.3 9.8 %collective-permute-done.8 = bf16[1024,256]{0,1:T(8,128)(2,1)S(1)} collective-permute-done((bf16[1024,256]{0,1:T(8,128)(2,1)S(1)}, bf16[1024,256]{0,1:T(8,128)(2,1)S(1)}, u32[]{:S(2)}, u32[]{:S(2)}) %collective-permute-start.8) | collective-permute-done | bytes 524320 | tf_op jit(solution)/shard_map/ppermute | solution.py:36
  147.9 16.2 %collective-permute-done.9 = bf16[1024,256]{0,1:T(8,128)(2,1)S(1)} collective-permute-done((bf16[1024,256]{0,1:T(8,128)(2,1)S(1)}, bf16[1024,256]{0,1:T(8,128)(2,1)S(1)}, u32[]{:S(2)}, u32[]{:S(2)}) %collective-permute-start.9) | collective-permute-done | bytes 524320 | tf_op jit(solution)/shard_map/ppermute | solution.py:36
  165.3 14.6 %collective-permute-done.10 = bf16[1024,256]{0,1:T(8,128)(2,1)S(1)} collective-permute-done((bf16[1024,256]{0,1:T(8,128)(2,1)S(1)}, bf16[1024,256]{0,1:T(8,128)(2,1)S(1)}, u32[]{:S(2)}, u32[]{:S(2)}) %collective-permute-start.10) | collective-permute-done | bytes 524320 | tf_op jit(solution)/shard_map/ppermute | solution.py:36
  181.4 9.5 %collective-permute-done.11 = bf16[1024,256]{0,1:T(8,128)(2,1)S(1)} collective-permute-done((bf16[1024,256]{0,1:T(8,128)(2,1)S(1)}, bf16[1024,256]{0,1:T(8,128)(2,1)S(1)}, u32[]{:S(2)}, u32[]{:S(2)}) %collective-permute-start.11) | collective-permute-done | bytes 524320 | tf_op jit(solution)/shard_map/ppermute | solution.py:36
  193.6 12.9 %psum.14 = f32[2,1024]{1,0:T(2,128)S(1)} all-reduce(f32[2,1024]{1,0:T(2,128)S(1)} %pad_maximum_fusion), channel_id=1, replica_groups=mesh['cells'=8,'genes'=4] {'cells'}, use_global_device_ids=true, to_apply=%region_6.0 | all-reduce | flops 2048 | bytes 16384 | tf_op jit(solution)/shard_map/psum | solution.py:43
  206.5 13.1 %all_gather.3 = f32[2,4096]{1,0:T(2,128)S(1)} all-gather(f32[2,1024]{1,0:T(2,128)S(1)} %psum.14), channel_id=1, replica_groups=mesh['cells'=8,'genes'=4] {'genes'}, dimensions={1}, use_global_device_ids=true | all-gather | bytes 40960 | tf_op jit(solution)/shard_map/all_gather | solution.py:44
  219.8 5.6 %reduce-scatter.9.cloned.1.call-done = f32[128,1024]{1,0:T(8,128)} async-done(((f32[1024,1024]{1,0:T(8,128)}), f32[128,1024]{1,0:T(8,128)}) %reduce-scatter.9.cloned.1.call-update) | async-done | bytes 524304 | tf_op jit(solution)/shard_map/reduce_scatter | solution.py:56
  225.4 54.4 %reduce-scatter.11.cloned.1.call-done = f32[128,1024]{1,0:T(8,128)} async-done(((f32[1024,1024]{1,0:T(8,128)}), f32[128,1024]{1,0:T(8,128)}) %reduce-scatter.11.cloned.1.call-update) | async-done | bytes 524304 | tf_op jit(solution)/shard_map/reduce_scatter | solution.py:56
  279.8 3.7 %fusion.23 = (f32[512]{0:T(512)S(1)}, f32[512,1024]{1,0:T(8,128)}) fusion(f32[1024]{0:T(1024)S(1)} %bitcast.121, f32[512]{0:T(512)S(1)} %bitcast.125, f32[1024]{0:T(1024)S(1)} %bitcast.122, f32[512]{0:T(512)S(1)} %bitcast.126, f32[128,1024]{1,0:T(8,128)} %reduce-scatter.11.cloned.1.call-done, f32[128,1024]{1,0:T(8,128)} %reduce-scatter.9.cloned.1.call-done, ...), kind=kLoop, calls=%fused_computation.55 | loop fusion | flops 7339520 | bytes 4214784 | tf_op jit(solution)/shard_map/reduce_sum | solution.py:77
  283.5 12.3 %psum.15 = f32[512]{0:T(512)} all-reduce(f32[512]{0:T(512)S(1)} %get-tuple-element.22), channel_id=1, replica_groups=mesh['cells'=8,'genes'=4] {'genes'}, use_global_device_ids=true, to_apply=%region_8.9 | all-reduce | flops 512 | bytes 4096 | tf_op jit(solution)/shard_map/psum | solution.py:77
  (56 shorter events, 30.1 us)
Async XLA Ops:
  7.2 5.4 %copy-start.4 = (s32[1024]{0:T(1024)S(1)}, s32[1024]{0:T(1024)}, u32[]{:S(2)}) copy-start(s32[1024]{0:T(1024)} %param.3) | copy-start | bytes 12292
  7.2 212.6 %reduce-scatter.5.cloned.1.call-start = ((), (), s32[]{:S(2)}) async-start(), calls=%async_computation.4 | async-start | bytes 4718592 | tf_op jit(solution)/shard_map/reduce_scatter | solution.py:56
  17.9 0.8 copy-start.2
  18.7 17.1 %collective-permute-start = (bf16[1024,256]{0,1:T(8,128)(2,1)S(1)}, bf16[1024,256]{0,1:T(8,128)(2,1)}, u32[]{:S(2)}, u32[]{:S(2)}) collective-permute-start(bf16[1024,256]{0,1:T(8,128)(2,1)S(1)} %bitcast.119), channel_id=1, source_target_pairs={{0,1},{1,2},{2,3},{3,0},{4,5},{5,6},{6,7},{7,4},{8,9},{9,10},{10,1... | collective-permute-start | bytes 1572872 | tf_op jit(solution)/shard_map/ppermute | solution.py:36
  35.8 15.2 %collective-permute-start.1 = (bf16[1024,256]{0,1:T(8,128)(2,1)}, bf16[1024,256]{0,1:T(8,128)(2,1)}, u32[]{:S(2)}, u32[]{:S(2)}) collective-permute-start(bf16[1024,256]{0,1:T(8,128)(2,1)} %collective-permute-done), channel_id=1, source_target_pairs={{0,1},{1,2},{2,3},{3,0},{4,5},{5,6},{6,7},{7,4},{8,9},{9,10},{10,1... | collective-permute-start | bytes 1572872 | tf_op jit(solution)/shard_map/ppermute | solution.py:36
  35.8 2.5 copy-start.3
  51.0 14.2 %collective-permute-start.2 = (bf16[1024,256]{0,1:T(8,128)(2,1)}, bf16[1024,256]{0,1:T(8,128)(2,1)S(1)}, u32[]{:S(2)}, u32[]{:S(2)}) collective-permute-start(bf16[1024,256]{0,1:T(8,128)(2,1)} %collective-permute-done.1), channel_id=1, source_target_pairs={{0,1},{1,2},{2,3},{3,0},{4,5},{5,6},{6,7},{7,4},{8,9},{9,10},{10,1... | collective-permute-start | bytes 1572872 | tf_op jit(solution)/shard_map/ppermute | solution.py:36
  67.0 152.8 %reduce-scatter.7.cloned.1.call-start = ((), (), s32[]{:S(2)}) async-start(), calls=%async_computation.5 | async-start | bytes 4718592 | tf_op jit(solution)/shard_map/reduce_scatter | solution.py:56
  67.0 15.9 %copy-start.1 = (bf16[1024,2,1,128]{0,3,2,1:T(8,128)(2,1)S(1)}, bf16[1024,2,1,128]{0,3,2,1:T(8,128)(2,1)}, u32[]{:S(2)}) copy-start(bf16[1024,2,1,128]{0,3,2,1:T(8,128)(2,1)} %get-tuple-element.28) | copy-start | bytes 1572868
  67.1 13.4 %collective-permute-start.3 = (bf16[1024,256]{0,1:T(8,128)(2,1)}, bf16[1024,256]{0,1:T(8,128)(2,1)S(1)}, u32[]{:S(2)}, u32[]{:S(2)}) collective-permute-start(bf16[1024,256]{0,1:T(8,128)(2,1)} %bitcast.117), channel_id=1, source_target_pairs={{0,1},{1,2},{2,3},{3,0},{4,5},{5,6},{6,7},{7,4},{8,9},{9,10},{10,1... | collective-permute-start | bytes 1572872 | tf_op jit(solution)/shard_map/ppermute | solution.py:36
  80.5 12.3 %collective-permute-start.4 = (bf16[1024,256]{0,1:T(8,128)(2,1)S(1)}, bf16[1024,256]{0,1:T(8,128)(2,1)S(1)}, u32[]{:S(2)}, u32[]{:S(2)}) collective-permute-start(bf16[1024,256]{0,1:T(8,128)(2,1)S(1)} %collective-permute-done.3), channel_id=1, source_target_pairs={{0,1},{1,2},{2,3},{3,0},{4,5},{5,6},{6,7},{7,4},{8,9},{9,10},{10,1... | collective-permute-start | bytes 1572872 | tf_op jit(solution)/shard_map/ppermute | solution.py:36
  92.8 11.5 %collective-permute-start.5 = (bf16[1024,256]{0,1:T(8,128)(2,1)S(1)}, bf16[1024,256]{0,1:T(8,128)(2,1)S(1)}, u32[]{:S(2)}, u32[]{:S(2)}) collective-permute-start(bf16[1024,256]{0,1:T(8,128)(2,1)S(1)} %collective-permute-done.4), channel_id=1, source_target_pairs={{0,1},{1,2},{2,3},{3,0},{4,5},{5,6},{6,7},{7,4},{8,9},{9,10},{10,1... | collective-permute-start | bytes 1572872 | tf_op jit(solution)/shard_map/ppermute | solution.py:36
  106.0 119.4 %reduce-scatter.9.cloned.1.call-start = ((), (), s32[]{:S(2)}) async-start(), calls=%async_computation.6 | async-start | bytes 4718592 | tf_op jit(solution)/shard_map/reduce_scatter | solution.py:56
  106.1 12.8 %collective-permute-start.6 = (bf16[1024,256]{0,1:T(8,128)(2,1)S(1)}, bf16[1024,256]{0,1:T(8,128)(2,1)S(1)}, u32[]{:S(2)}, u32[]{:S(2)}) collective-permute-start(bf16[1024,256]{0,1:T(8,128)(2,1)S(1)} %bitcast.115), channel_id=1, source_target_pairs={{0,1},{1,2},{2,3},{3,0},{4,5},{5,6},{6,7},{7,4},{8,9},{9,10},{10,1... | collective-permute-start | bytes 1572872 | tf_op jit(solution)/shard_map/ppermute | solution.py:36
  118.9 13.9 %collective-permute-start.7 = (bf16[1024,256]{0,1:T(8,128)(2,1)S(1)}, bf16[1024,256]{0,1:T(8,128)(2,1)S(1)}, u32[]{:S(2)}, u32[]{:S(2)}) collective-permute-start(bf16[1024,256]{0,1:T(8,128)(2,1)S(1)} %collective-permute-done.6), channel_id=1, source_target_pairs={{0,1},{1,2},{2,3},{3,0},{4,5},{5,6},{6,7},{7,4},{8,9},{9,10},{10,1... | collective-permute-start | bytes 1572872 | tf_op jit(solution)/shard_map/ppermute | solution.py:36
  132.8 13.2 %collective-permute-start.8 = (bf16[1024,256]{0,1:T(8,128)(2,1)S(1)}, bf16[1024,256]{0,1:T(8,128)(2,1)S(1)}, u32[]{:S(2)}, u32[]{:S(2)}) collective-permute-start(bf16[1024,256]{0,1:T(8,128)(2,1)S(1)} %collective-permute-done.7), channel_id=1, source_target_pairs={{0,1},{1,2},{2,3},{3,0},{4,5},{5,6},{6,7},{7,4},{8,9},{9,10},{10,1... | collective-permute-start | bytes 1572872 | tf_op jit(solution)/shard_map/ppermute | solution.py:36
  147.7 132.0 %reduce-scatter.11.cloned.1.call-start = ((), (), s32[]{:S(2)}) async-start(), calls=%async_computation.7 | async-start | bytes 4718592 | tf_op jit(solution)/shard_map/reduce_scatter | solution.py:56
  147.8 16.2 %collective-permute-start.9 = (bf16[1024,256]{0,1:T(8,128)(2,1)S(1)}, bf16[1024,256]{0,1:T(8,128)(2,1)S(1)}, u32[]{:S(2)}, u32[]{:S(2)}) collective-permute-start(bf16[1024,256]{0,1:T(8,128)(2,1)S(1)} %bitcast.113), channel_id=1, source_target_pairs={{0,1},{1,2},{2,3},{3,0},{4,5},{5,6},{6,7},{7,4},{8,9},{9,10},{10,1... | collective-permute-start | bytes 1572872 | tf_op jit(solution)/shard_map/ppermute | solution.py:36
  164.0 15.8 %collective-permute-start.10 = (bf16[1024,256]{0,1:T(8,128)(2,1)S(1)}, bf16[1024,256]{0,1:T(8,128)(2,1)S(1)}, u32[]{:S(2)}, u32[]{:S(2)}) collective-permute-start(bf16[1024,256]{0,1:T(8,128)(2,1)S(1)} %collective-permute-done.9), channel_id=1, source_target_pairs={{0,1},{1,2},{2,3},{3,0},{4,5},{5,6},{6,7},{7,4},{8,9},{9,10},{10,1... | collective-permute-start | bytes 1572872 | tf_op jit(solution)/shard_map/ppermute | solution.py:36
  179.9 11.0 %collective-permute-start.11 = (bf16[1024,256]{0,1:T(8,128)(2,1)S(1)}, bf16[1024,256]{0,1:T(8,128)(2,1)S(1)}, u32[]{:S(2)}, u32[]{:S(2)}) collective-permute-start(bf16[1024,256]{0,1:T(8,128)(2,1)S(1)} %collective-permute-done.10), channel_id=1, source_target_pairs={{0,1},{1,2},{2,3},{3,0},{4,5},{5,6},{6,7},{7,4},{8,9},{9,10},{10,1... | collective-permute-start | bytes 1572872 | tf_op jit(solution)/shard_map/ppermute | solution.py:36
  191.6 1.9 copy-start
Sparse Core Ops, SparseCore 0:
  67.1 48.8 reduce-scatter.4
  119.4 51.1 reduce-scatter.6
  173.9 51.4 reduce-scatter.8
  228.6 51.1 reduce-scatter.10

commit v2 on v1

v2 whole, which is shorter than its diff:
```python
import functools

import jax
import jax.numpy as jnp
from jax import lax
from jax.experimental import pallas as pl
from jax.experimental.pallas import tpu as pltpu
from jax.sharding import PartitionSpec as P

CHUNKS = 4
TILE = 256


def bit(value, index):
    return (value // (1 << index)) % 2


def flip(value, index):
    return value + (1 << index) * (1 - 2 * bit(value, index))


def network(cell_groups, gene_groups, owners, xq_ref, own_ref, sums_ref, out_ref, stats_ref,
            held, partial, landed, totals, sums_in,
            ring_send, ring_recv, cut_send, cut_recv, fly_send, fly_recv, stat_send, stat_recv):
    chunks, rows, cells = xq_ref.shape
    part = rows // owners
    cols = own_ref.shape[1]
    half = cols // 2
    c = lax.axis_index("cells")
    g = lax.axis_index("genes")
    right = lax.rem(g + 1, gene_groups)
    left = lax.rem(g + gene_groups - 1, gene_groups)
    bits = cell_groups.bit_length() - 1
    hops = gene_groups - 1
    orders = (tuple(range(bits)), (0,) + tuple(range(bits - 1, 0, -1)))

    barrier = pltpu.get_barrier_semaphore()
    for target in [(c, left), (c, right)] + [(flip(c, b), g) for b in range(bits)]:
        pl.semaphore_signal(barrier, inc=1, device_id=target, device_id_type=pl.DeviceIdType.MESH)
    pl.semaphore_wait(barrier, 2 + bits)

    def ring(q, hop, piece):
        span = pl.ds(piece * (rows // 2), rows // 2)
        source = xq_ref.at[q, span] if hop == 0 else held.at[q, hop - 1, span]
        return pltpu.make_async_remote_copy(
            src_ref=source, dst_ref=held.at[q, hop, span],
            send_sem=ring_send.at[q, hop, piece], recv_sem=ring_recv.at[q, hop, piece],
            device_id=(c, right), device_id_type=pl.DeviceIdType.MESH)

    def cut(q, side, stage):
        count = cell_groups >> (stage + 1)
        return pltpu.make_async_remote_copy(
            src_ref=partial.at[q, side, pl.ds(count, count)],
            dst_ref=landed.at[q, side, pl.ds(count, count)],
            send_sem=cut_send.at[q, side, stage], recv_sem=cut_recv.at[q, side, stage],
            device_id=(flip(c, orders[side][stage]), g), device_id_type=pl.DeviceIdType.MESH)

    def fly(stage):
        return pltpu.make_async_remote_copy(
            src_ref=totals.at[stage], dst_ref=sums_in.at[stage],
            send_sem=fly_send.at[stage], recv_sem=fly_recv.at[stage],
            device_id=(flip(c, stage), g), device_id_type=pl.DeviceIdType.MESH)

    def spread(hop):
        source = totals.at[bits] if hop == 0 else stats_ref.at[hop]
        return pltpu.make_async_remote_copy(
            src_ref=source, dst_ref=stats_ref.at[hop + 1],
            send_sem=stat_send.at[hop], recv_sem=stat_recv.at[hop],
            device_id=(c, right), device_id_type=pl.DeviceIdType.MESH)

    def place(owner, side):
        total = 0
        for position, b in enumerate(orders[side]):
            total = total + ((bit(owner, b) + bit(c, b)) % 2) * (1 << (bits - 1 - position))
        return total

    def multiply(q, step):
        source = lax.rem(g - step + gene_groups, gene_groups)
        block = xq_ref.at[q] if step == 0 else held.at[q, step - 1]
        for side in range(2):
            spots = [place(source * owners + o, side) for o in range(owners)]

            @pl.loop(0, half // TILE)
            def _(t):
                start = pl.multiple_of(t * TILE, TILE)
                columns = pl.ds(pl.multiple_of(side * half + start, TILE), TILE)
                tile = jnp.dot(block[...], own_ref[:, columns], preferred_element_type=jnp.float32)
                for o in range(owners):
                    partial[q, side, spots[o], :, pl.ds(start, TILE)] = tile[o * part:(o + 1) * part]

    def launch(q, stage):
        for side in range(2):
            cut(q, side, stage).start()

    def absorb(q, stage):
        count = cell_groups >> (stage + 1)
        for side in range(2):
            cut(q, side, stage).wait_recv()
            if count > 1:
                @pl.loop(0, count)
                def _(i):
                    partial[q, side, i] = partial[q, side, i] + landed[q, side, i + count]
            else:
                out_ref[pl.ds(q * part, part), side * half:(side + 1) * half] = (
                    partial[q, side, 0] + landed[q, side, 1])

    for piece in range(2):
        ring(0, 0, piece).start()
    totals[0] = sums_ref[...]
    for stage in range(bits):
        fly(stage).start()
        fly(stage).wait_recv()
        totals[stage + 1] = totals[stage] + sums_in[stage]
    stats_ref[0] = totals[bits]

    turns = [[s for s in range(bits) if s * hops // bits == h] for h in range(hops)]

    @pl.loop(0, chunks)
    def _(q):
        multiply(q, 0)
        for hop in range(hops):
            for piece in range(2):
                ring(q, hop, piece).wait_recv()
                if hop < hops - 1:
                    ring(q, hop + 1, piece).start()
            if hop == max(hops - 2, 0):
                @pl.when(q < chunks - 1)
                def _():
                    for piece in range(2):
                        ring(q + 1, 0, piece).start()

            @pl.when(q > 0)
            def _():
                for stage in turns[hop]:
                    absorb(q - 1, stage)
                    if stage + 1 < bits:
                        launch(q - 1, stage + 1)
            multiply(q, hop + 1)
        launch(q, 0)

    last = chunks - 1
    spread(0).start()
    for stage in range(bits):
        absorb(last, stage)
        if stage + 1 < bits:
            launch(last, stage + 1)
        if stage < hops:
            spread(stage).wait_recv()
            if stage + 1 < hops:
                spread(stage + 1).start()
    for hop in range(bits, hops):
        spread(hop).wait_recv()
        if hop + 1 < hops:
            spread(hop + 1).start()
    for hop in range(hops):
        spread(hop).wait_send()
    for stage in range(bits):
        fly(stage).wait_send()

    @pl.loop(0, chunks)
    def _(q):
        for hop in range(hops):
            for piece in range(2):
                ring(q, hop, piece).wait_send()
        for side in range(2):
            for stage in range(bits):
                cut(q, side, stage).wait_send()


def normalize(counts, library):
    factor = 10000.0 / library.astype(jnp.float32)
    return jnp.log1p(counts.astype(jnp.float32) * factor[:, None]).astype(jnp.bfloat16)


def shards(counts, library):
    own_block = normalize(counts, library)
    cells, col_width = own_block.shape
    cell_groups = lax.axis_size("cells")
    gene_groups = lax.axis_size("genes")
    row_width = col_width * gene_groups // cell_groups
    owners = col_width // row_width
    part = row_width // CHUNKS
    total_cells = float(cells * cell_groups)
    me = lax.axis_index("genes")

    transposed = own_block.T.reshape(owners, CHUNKS, part, cells)
    ordered = jnp.transpose(transposed, (1, 0, 2, 3)).reshape(CHUNKS, owners * part, cells)
    widened = own_block.astype(jnp.float32)
    sums = jnp.stack([jnp.sum(widened, axis=0), jnp.sum(widened * widened, axis=0)])
    sums = jnp.concatenate([sums, jnp.zeros((6, col_width), jnp.float32)], axis=0)
    bits = cell_groups.bit_length() - 1
    hops = gene_groups - 1
    vmem = pl.BlockSpec(memory_space=pltpu.VMEM)
    dma = pltpu.SemaphoreType.DMA
    gram_tile, stats = pl.pallas_call(
        functools.partial(network, cell_groups, gene_groups, owners),
        out_shape=(
            jax.ShapeDtypeStruct((row_width, col_width), jnp.float32),
            jax.ShapeDtypeStruct((gene_groups, 8, col_width), jnp.float32),
        ),
        in_specs=[vmem] * 3,
        out_specs=(vmem, vmem),
        scratch_shapes=[
            pltpu.VMEM((CHUNKS, hops, owners * part, cells), jnp.bfloat16),
            pltpu.VMEM((CHUNKS, 2, cell_groups, part, col_width // 2), jnp.float32),
            pltpu.VMEM((CHUNKS, 2, cell_groups, part, col_width // 2), jnp.float32),
            pltpu.VMEM((bits + 1, 8, col_width), jnp.float32),
            pltpu.VMEM((bits, 8, col_width), jnp.float32),
            dma((CHUNKS, hops, 2)), dma((CHUNKS, hops, 2)),
            dma((CHUNKS, 2, bits)), dma((CHUNKS, 2, bits)),
            dma((bits,)), dma((bits,)),
            dma((hops,)), dma((hops,)),
        ],
        compiler_params=pltpu.CompilerParams(
            collective_id=0, has_side_effects=True, vmem_limit_bytes=60 * 1024 * 1024),
    )(ordered, own_block, sums)
    order = lax.rem(me - jnp.arange(gene_groups) + gene_groups, gene_groups)
    all_sums = jnp.transpose(jnp.take(stats[:, :2], order, axis=0), (1, 0, 2)).reshape(2, -1)

    means = all_sums[0] / total_cells
    variances = all_sums[1] / total_cells - means * means
    scales = lax.rsqrt(variances + 1e-05)
    row_first = lax.axis_index("cells") * row_width
    col_first = me * col_width
    row_means = lax.dynamic_slice_in_dim(means, row_first, row_width, 0)
    col_means = lax.dynamic_slice_in_dim(means, col_first, col_width, 0)
    row_scales = lax.dynamic_slice_in_dim(scales, row_first, row_width, 0)
    col_scales = lax.dynamic_slice_in_dim(scales, col_first, col_width, 0)
    correlation = (
        (gram_tile / total_cells - row_means[:, None] * col_means[None, :])
        * row_scales[:, None]
        * col_scales[None, :]
    )
    powered = correlation**6
    row_index = row_first + jnp.arange(row_width, dtype=jnp.int32)[:, None]
    col_index = col_first + jnp.arange(col_width, dtype=jnp.int32)[None, :]
    adjacency = jnp.where(row_index == col_index, jnp.float32(0.0), powered)
    connectivity = lax.psum(jnp.sum(adjacency, axis=1), "genes")
    return (adjacency, connectivity)


def solution(mesh):
    return jax.shard_map(
        shards,
        mesh=mesh,
        in_specs=(P("cells", "genes"), P("cells")),
        out_specs=(P("cells", "genes"), P("cells")),
        check_vma=False,
    )
```

time: 303 us -> 202 us (0.67)
  waiting for transfers between devices: 196 us -> 0 us
  Pallas kernels: 0 us -> 173 us
  blocking collectives: 38.3 us -> 9.55 us
  matrix products: 25.9 us -> 0 us
  between operations: 13.9 us -> 0.73 us
  local copies, waits for them, and re-layouts: 17.1 us -> 8.77 us
  starting transfers between devices: 3.41 us -> 0 us
    pallas_call x0 -> x1, Pallas kernels: none -> 173 us  [shards(): pl.pallas_call(functools.partial(network, cell_groups, gene_groups, owner...]
    ppermute x12 -> x0, waiting for transfers between devices: 135 us -> none  [shards(): held = lax.ppermute(held, 'genes', ring)]
    reduce_scatter x4 -> x0, waiting for transfers between devices: 60 us -> none  [shards(): lax.psum_scatter(tiles, 'cells', scatter_dimension=0, tiled=True)]
    dot_general x16 -> x0, matrix products: 25.9 us -> none  [shards(): lax.dot_general(blocks[q][step], own_block, (((0,), (0,)), ((), ())), pre...]
    all_gather x1 -> x0, blocking collectives: 13.1 us -> none  [shards(): all_sums = lax.all_gather(sums, 'genes', axis=1, tiled=True)]
    psum x1 -> x0, blocking collectives: 12.9 us -> none  [shards(): sums = lax.psum(sums, 'cells')]
    unnamed x11 -> x2, local copies, waits for them, and re-layouts: 8.11 us -> 0.01 us
    another operation x4 -> x0, local copies, waits for them, and re-layouts: 7.97 us -> none
  transfers between devices with their start and end apart: 16 -> 0, of which waited for: 14 -> 0; matrix products, arithmetic and copies ran while one was open for 11% -> 0% of each run, Pallas kernels for 0% -> 0%
where the time goes in v2:
time: 202 us; the launch traced here: 201 us
  Pallas kernels  173 us (86%)
  other arithmetic  9.74 us (5%)
  blocking collectives  9.55 us (5%)
  local copies, waits for them, and re-layouts  8.77 us (4%)
    pallas_call x1, Pallas kernels, shards(): pl.pallas_call(functools.partial(network, cell_groups, gene_groups, owner...  173 us
    psum x1, blocking collectives, shards(): connectivity = lax.psum(jnp.sum(adjacency, axis=1), 'genes')  9.55 us
    transpose x1, local copies, waits for them, and re-layouts, shards(): jnp.transpose(transposed, (1, 0, 2, 3))  4.34 us
    reduce_sum x1, other arithmetic, shards(): jnp.sum(widened, axis=0)  4.25 us

profile of v2, /device:TPU:0, one launch (start us, length us, event | category | flops | bytes accessed | tf_op | source)
XLA Modules:
  0.0 201.5 jit_solution(16698583057463358565)
XLA Ops:
  0.6 0.7 convert_divide_fusion
  1.3 4.2 %convert_reduce_fusion = (f32[1024]{0:T(1024)S(1)}, f32[1024]{0:T(1024)S(1)}, bf16[1024,1024]{1,0:T(8,128)(2,1)S(1)}) fusion(f32[1024]{0:T(1024)S(1)} %convert_divide_fusion, s32[1024,1024]{1,0:T(8,128)} %param.2), kind=kLoop, calls=%fused_computation.2 | loop fusion | flops 7337984 | bytes 6303744 | tf_op jit(solution)/shard_map/reduce_sum | solution.py:189
  5.6 0.0 copy-start
  5.6 0.1 pad.2.clone
  5.7 0.9 maximum_maximum_fusion.sums_ref
  6.5 2.7 %reshape.76 = bf16[2,4,128,1024]{2,1,0,3:T(4,128)(2,1)} reshape(bf16[1024,1024]{0,1:T(8,128)(2,1)S(1)} %bitcast.13) | data formatting | bytes 4194304 | tf_op jit(solution)/shard_map/reshape | solution.py:186
  9.2 0.0 copy-done
  9.2 4.3 %copy.4 = bf16[4,2,128,1024]{3,2,1,0:T(8,128)(2,1)} copy(bf16[4,2,128,1024]{2,0,1,3:T(4,128)(2,1)} %bitcast.15) | data formatting | bytes 4194304 | tf_op jit(solution)/shard_map/transpose | solution.py:187
  13.6 172.7 %shard_map.41 = (f32[512,1024]{1,0:T(8,128)}, f32[4,8,1024]{2,1,0:T(8,128)}) custom-call(bf16[4,256,1024]{2,1,0:T(8,128)(2,1)} %bitcast.14, bf16[1024,1024]{1,0:T(8,128)(2,1)} %copy-done, f32[8,1024]{1,0:T(8,128)} %maximum_maximum_fusion.sums_ref), custom_call_target="tpu_custom_call" | custom-call | tf_op jit(solution)/shard_map/pallas_call | solution.py:195
  186.3 0.9 slice.11
  187.2 0.6 gather_fusion
  187.8 0.1 select_bitcast_fusion
  188.0 0.1 dynamic_slice.14
  188.1 0.1 dynamic_slice.12
  188.1 3.8 %fusion.5 = (f32[512]{0:T(512)S(1)}, f32[512,1024]{1,0:T(8,128)}) fusion(f32[1024]{0:T(1024)S(1)} %dynamic_slice.15, f32[512]{0:T(512)S(1)} %dynamic_slice.14, f32[1024]{0:T(1024)S(1)} %dynamic_slice.13, f32[512]{0:T(512)S(1)} %dynamic_slice.12, f32[512,1024]{1,0:T(8,128)} %get-tuple-element.4, s32[1024]{0:T(1024)S(1)} %iota_add_fusion, ...), kind=kLoop, calls=%fused_computation.26 | loop fusion | flops 5766656 | bytes 4214784 | tf_op jit(solution)/shard_map/reduce_sum | solution.py:238
  191.9 9.6 %psum.7 = f32[512]{0:T(512)} all-reduce(f32[512]{0:T(512)S(1)} %get-tuple-element.8), channel_id=1, replica_groups=mesh['cells'=8,'genes'=4] {'genes'}, use_global_device_ids=true, to_apply=%region_3.4 | all-reduce | flops 512 | bytes 4096 | tf_op jit(solution)/shard_map/psum | solution.py:238
  (10 shorter events, 0.1 us)
Async XLA Ops:
  5.6 3.7 %copy-start = (bf16[1024,1024]{1,0:T(8,128)(2,1)}, bf16[1024,1024]{1,0:T(8,128)(2,1)S(1)}, u32[]{:S(2)}) copy-start(bf16[1024,1024]{1,0:T(8,128)(2,1)S(1)} %get-tuple-element.10.own_ref) | copy-start | bytes 6291460

commit v3 on v2

--- a/solution.py
+++ b/solution.py
@@ -7,8 +7,8 @@
 from jax.experimental.pallas import tpu as pltpu
 from jax.sharding import PartitionSpec as P
 
-CHUNKS = 4
-TILE = 256
+CHUNKS = 8
+TILE = 512
 
 
 def bit(value, index):
@@ -19,11 +19,11 @@
     return value + (1 << index) * (1 - 2 * bit(value, index))
 
 
-def network(cell_groups, gene_groups, owners, xq_ref, own_ref, sums_ref, out_ref, stats_ref,
+def network(cell_groups, gene_groups, xq_ref, own_ref, sums_ref, out_ref, stats_ref,
             held, partial, landed, totals, sums_in,
             ring_send, ring_recv, cut_send, cut_recv, fly_send, fly_recv, stat_send, stat_recv):
-    chunks, rows, cells = xq_ref.shape
-    part = rows // owners
+    owners, chunks, part, cells = xq_ref.shape
+    rows = owners * part
     cols = own_ref.shape[1]
     half = cols // 2
     c = lax.axis_index("cells")
@@ -40,8 +40,8 @@
     pl.semaphore_wait(barrier, 2 + bits)
 
     def ring(q, hop, piece):
-        span = pl.ds(piece * (rows // 2), rows // 2)
-        source = xq_ref.at[q, span] if hop == 0 else held.at[q, hop - 1, span]
+        span = pl.ds(piece * (owners // 2), owners // 2)
+        source = xq_ref.at[span, q] if hop == 0 else held.at[q, hop - 1, span]
         return pltpu.make_async_remote_copy(
             src_ref=source, dst_ref=held.at[q, hop, span],
             send_sem=ring_send.at[q, hop, piece], recv_sem=ring_recv.at[q, hop, piece],
@@ -76,7 +76,7 @@
 
     def multiply(q, step):
         source = lax.rem(g - step + gene_groups, gene_groups)
-        block = xq_ref.at[q] if step == 0 else held.at[q, step - 1]
+        block = xq_ref.at[:, q] if step == 0 else held.at[q, step - 1]
         for side in range(2):
             spots = [place(source * owners + o, side) for o in range(owners)]
 
@@ -84,7 +84,7 @@
             def _(t):
                 start = pl.multiple_of(t * TILE, TILE)
                 columns = pl.ds(pl.multiple_of(side * half + start, TILE), TILE)
-                tile = jnp.dot(block[...], own_ref[:, columns], preferred_element_type=jnp.float32)
+                tile = jnp.dot(block[...].reshape(rows, cells), own_ref[:, columns], preferred_element_type=jnp.float32)
                 for o in range(owners):
                     partial[q, side, spots[o], :, pl.ds(start, TILE)] = tile[o * part:(o + 1) * part]
 
@@ -179,12 +179,12 @@
     gene_groups = lax.axis_size("genes")
     row_width = col_width * gene_groups // cell_groups
     owners = col_width // row_width
-    part = row_width // CHUNKS
     total_cells = float(cells * cell_groups)
     me = lax.axis_index("genes")
 
-    transposed = own_block.T.reshape(owners, CHUNKS, part, cells)
-    ordered = jnp.transpose(transposed, (1, 0, 2, 3)).reshape(CHUNKS, owners * part, cells)
+    chunks = min(CHUNKS, row_width // 16)
+    part = row_width // chunks
+    ordered = own_block.T.reshape(owners, chunks, part, cells)
     widened = own_block.astype(jnp.float32)
     sums = jnp.stack([jnp.sum(widened, axis=0), jnp.sum(widened * widened, axis=0)])
     sums = jnp.concatenate([sums, jnp.zeros((6, col_width), jnp.float32)], axis=0)
@@ -193,7 +193,7 @@
     vmem = pl.BlockSpec(memory_space=pltpu.VMEM)
     dma = pltpu.SemaphoreType.DMA
     gram_tile, stats = pl.pallas_call(
-        functools.partial(network, cell_groups, gene_groups, owners),
+        functools.partial(network, cell_groups, gene_groups),
         out_shape=(
             jax.ShapeDtypeStruct((row_width, col_width), jnp.float32),
             jax.ShapeDtypeStruct((gene_groups, 8, col_width), jnp.float32),
@@ -201,13 +201,13 @@
         in_specs=[vmem] * 3,
         out_specs=(vmem, vmem),
         scratch_shapes=[
-            pltpu.VMEM((CHUNKS, hops, owners * part, cells), jnp.bfloat16),
-            pltpu.VMEM((CHUNKS, 2, cell_groups, part, col_width // 2), jnp.float32),
-            pltpu.VMEM((CHUNKS, 2, cell_groups, part, col_width // 2), jnp.float32),
+            pltpu.VMEM((chunks, hops, owners, part, cells), jnp.bfloat16),
+            pltpu.VMEM((chunks, 2, cell_groups, part, col_width // 2), jnp.float32),
+            pltpu.VMEM((chunks, 2, cell_groups, part, col_width // 2), jnp.float32),
             pltpu.VMEM((bits + 1, 8, col_width), jnp.float32),
             pltpu.VMEM((bits, 8, col_width), jnp.float32),
-            dma((CHUNKS, hops, 2)), dma((CHUNKS, hops, 2)),
-            dma((CHUNKS, 2, bits)), dma((CHUNKS, 2, bits)),
+            dma((chunks, hops, 2)), dma((chunks, hops, 2)),
+            dma((chunks, 2, bits)), dma((chunks, 2, bits)),
             dma((bits,)), dma((bits,)),
             dma((hops,)), dma((hops,)),
         ],

time: 202 us -> 189 us (0.936)
  Pallas kernels: 173 us -> 163 us
  local copies, waits for them, and re-layouts: 8.77 us -> 4.28 us
    pallas_call x1, Pallas kernels: 173 us -> 163 us  [shards(): pl.pallas_call(functools.partial(network, cell_groups, gene_groups), out_...]
    reshape x1 -> x0, local copies, waits for them, and re-layouts: 2.69 us -> none  [shards(): transposed = own_block.T.reshape(owners, CHUNKS, part, cells)]
where the time goes in v3:
time: 189 us; the launch traced here: 188 us
  Pallas kernels  163 us (86%)
  blocking collectives  10.4 us (6%)
  other arithmetic  9.71 us (5%)
  local copies, waits for them, and re-layouts  4.28 us (2%)
    pallas_call x1, Pallas kernels, shards(): pl.pallas_call(functools.partial(network, cell_groups, gene_groups), out_...  163 us
    psum x1, blocking collectives, shards(): connectivity = lax.psum(jnp.sum(adjacency, axis=1), 'genes')  10.4 us
    reduce_sum x1, other arithmetic, shards(): jnp.sum(widened, axis=0)  4.25 us

profile of v3, /device:TPU:0, one launch (start us, length us, event | category | flops | bytes accessed | tf_op | source)
XLA Modules:
  0.0 188.5 jit_solution(17764761418128290587)
XLA Ops:
  0.6 0.7 convert_divide_fusion
  1.3 4.2 %convert_reduce_fusion = (f32[1024]{0:T(1024)S(1)}, f32[1024]{0:T(1024)S(1)}, bf16[1024,1024]{1,0:T(8,128)(2,1)S(1)}) fusion(f32[1024]{0:T(1024)S(1)} %convert_divide_fusion, s32[1024,1024]{1,0:T(8,128)} %param.2), kind=kLoop, calls=%fused_computation.2 | loop fusion | flops 7337984 | bytes 6303744 | tf_op jit(solution)/shard_map/reduce_sum | solution.py:189
  5.6 0.0 copy-start
  5.6 0.1 pad.2.clone
  5.7 0.8 maximum_maximum_fusion.sums_ref
  6.5 2.5 %copy.5 = bf16[1024,1024]{1,0:T(8,128)(2,1)} copy(bf16[1024,1024]{0,1:T(8,128)(2,1)S(1)} %bitcast.10) | data formatting | bytes 4194304 | tf_op jit(solution)/shard_map/transpose | solution.py:187
  9.1 0.0 copy-done
  9.1 163.4 %shard_map.41 = (f32[512,1024]{1,0:T(8,128)}, f32[4,8,1024]{2,1,0:T(8,128)}) custom-call(bf16[2,8,64,1024]{3,2,1,0:T(8,128)(2,1)} %bitcast.11, bf16[1024,1024]{1,0:T(8,128)(2,1)} %copy-done, f32[8,1024]{1,0:T(8,128)} %maximum_maximum_fusion.sums_ref), custom_call_target="tpu_custom_call" | custom-call | tf_op jit(solution)/shard_map/pallas_call | solution.py:195
  172.4 0.9 slice.11
  173.4 0.6 gather_fusion
  174.0 0.1 select_bitcast_fusion
  174.2 0.1 dynamic_slice.14
  174.2 0.1 dynamic_slice.12
  174.3 3.8 %fusion.5 = (f32[512]{0:T(512)S(1)}, f32[512,1024]{1,0:T(8,128)}) fusion(f32[1024]{0:T(1024)S(1)} %dynamic_slice.15, f32[512]{0:T(512)S(1)} %dynamic_slice.14, f32[1024]{0:T(1024)S(1)} %dynamic_slice.13, f32[512]{0:T(512)S(1)} %dynamic_slice.12, f32[512,1024]{1,0:T(8,128)} %get-tuple-element.4, s32[1024]{0:T(1024)S(1)} %iota_add_fusion, ...), kind=kLoop, calls=%fused_computation.26 | loop fusion | flops 5766656 | bytes 4214784 | tf_op jit(solution)/shard_map/reduce_sum | solution.py:238
  178.1 10.4 %psum.7 = f32[512]{0:T(512)} all-reduce(f32[512]{0:T(512)S(1)} %get-tuple-element.8), channel_id=1, replica_groups=mesh['cells'=8,'genes'=4] {'genes'}, use_global_device_ids=true, to_apply=%region_3.4 | all-reduce | flops 512 | bytes 4096 | tf_op jit(solution)/shard_map/psum | solution.py:238
  (10 shorter events, 0.1 us)
Async XLA Ops:
  5.6 3.5 %copy-start = (bf16[1024,1024]{1,0:T(8,128)(2,1)}, bf16[1024,1024]{1,0:T(8,128)(2,1)S(1)}, u32[]{:S(2)}) copy-start(bf16[1024,1024]{1,0:T(8,128)(2,1)S(1)} %get-tuple-element.10.own_ref) | copy-start | bytes 6291460
